TPU v7x, 256 devices: a 8x8x2 block of a 8x8x16 slice. The times are simulated.
256 devices in a mesh: grp: 2 (over z), tp: 128 (over x, y, core).
Axes of the slice: x: 8, y: 8, z: 2, core: 2. Of those that a mesh axis runs over, the one named last changes fastest.
The devices are a block of a 8x8x16 slice.
Arguments:
- hidden_in: float32 [64, 4608], P('grp'), parts along dimension 0, may hold values from -6 to 6
- prefill_cache: bfloat16 [128, 1, 2, 4, 128, 8, 256], P('tp', None, None, 'grp'), parts along dimension 3, may hold values from -6 to 6
- lengths: int32 [64], P('grp'), parts along dimension 0, may hold values from 1 to 1023
- page_table: int32 [64, 128], P('grp'), parts along dimension 0, may hold values from 0 to 127, each once within a row
- qkv_weight: bfloat16 [1, 8192, 4608], P(None, 'tp'), may hold values from -0.09375 to 0.09375
- out_weight: bfloat16 [1, 4608, 4096], P(None, 'tp'), may hold values from -0.09375 to 0.09375
- gate_up_weight: bfloat16 [1, 2, 18432, 4608], P(None, None, 'tp'), may hold values from -0.09375 to 0.09375
- down_weight: bfloat16 [1, 18432, 4608], P(None, 'tp'), may hold values from -0.15625 to 0.15625
- norm_gains: float32 [1, 4, 4608], replicated, may hold values from 0.25 to 1.75
Outputs:
- hidden_out: float32 [64, 4608], P('grp', 'tp'), parts along dimension 0
- decode_cache: bfloat16 [128, 1, 2, 64, 8, 2048], P('tp', None, None, 'grp'), parts along dimension 3
There are 2 independent parts, one for each index of `grp`. A program takes and returns all parts, laid end to end along the dimension named above; an argument that names none is the same for every part. Nothing has to cross between parts.
Inputs may be any that keep to these rules, and one draw needn't show every extreme that they name: Request r's new token takes position lengths[r]. Each row is a permutation of 0 to 127; page j of request r holds cache positions page_table[r, j] * 8 to page_table[r, j] * 8 + 7.
All inputs are finite; a program needn't handle non-finite values.
Results may differ from a plain program's by a relative error of at most 0.012.
The roundings to bfloat16 on the way count: a program that leaves them out, or rounds other values in their place, can miss the bound.
Values may be sent and summed in bfloat16 or wider, within the bound.
A program may use at most 64 MiB of HBM per device.

v0:
```python
import jax
import jax.numpy as jnp
from jax import lax
from jax.sharding import Mesh
from jax.sharding import PartitionSpec as P

D = 4608
HEADS = 32
KV_HEADS = 16
HEAD_DIM = 128
PREFILL_TP = 8
TP = ("tp_0", "tp_1", "tp_2")
EPSILON = 1e-06
SOFTCAP = 50.0


def cut_along(shard, dim, size):
    before, after = (shard.shape[:dim], shard.shape[dim + 1 :])
    return jnp.moveaxis(shard.reshape(*before, size, -1, *after), dim, 0)


def joined_along(tiles, dim):
    tiles = jnp.moveaxis(tiles, 0, dim)
    shape = tiles.shape
    return tiles.reshape(*shape[:dim], shape[dim] * shape[dim + 1], *shape[dim + 2 :])


def turned_blocks(tiles, axes, turns):
    shape = [lax.axis_size(a) for a in axes]
    tiles = tiles.reshape(*shape, *tiles.shape[1:])
    for k in turns:
        tiles = lax.all_to_all(tiles, axes[k], split_axis=k, concat_axis=k, tiled=True)
    return tiles.reshape(-1, *tiles.shape[len(axes) :])


def exchange_by_chip(shard, groups, turns, split_dim, concat_dim):
    size = lax.axis_size(groups[0]) * lax.axis_size(groups[1])
    tiles = cut_along(shard, split_dim, size)
    return joined_along(turned_blocks(tiles, groups, turns), concat_dim)


def gather_in_order(shard, axes, turns):
    tiles = shard[None]
    for k in turns:
        tiles = lax.all_gather(tiles, axes[k], axis=0, tiled=True)
    held = [lax.axis_size(axes[k]) for k in reversed(turns)]
    tiles = tiles.reshape(*held, *shard.shape)
    turned = sorted(range(len(turns)), key=lambda place: turns[len(turns) - 1 - place])
    return tiles.transpose(*turned, *range(len(turns), tiles.ndim)).reshape(-1, *shard.shape)


def gather_axes(shard, axes, turns, dim):
    return joined_along(gather_in_order(shard, axes, turns), dim)


def own_block(tiles, axes, turns):
    shape = [lax.axis_size(a) for a in axes]
    tiles = tiles.reshape(*shape, *tiles.shape[1:])
    tiles = tiles.transpose(*turns, *range(len(axes), tiles.ndim))
    tiles = tiles.reshape(-1, *tiles.shape[len(axes) :])
    for k in turns:
        tiles = lax.psum_scatter(tiles, axes[k], scatter_dimension=0, tiled=True)
    return tiles[0]


def summed_rows(shard, axes, turns, dim):
    size = lax.axis_size(axes)
    return own_block(cut_along(shard, dim, size), axes, turns)


def one_axis_at_a_time(shard, axes):
    for axis in axes:
        shard = lax.psum(shard, axis)
    return shard


def rms_scale(vector, gain_row):
    meansq = jnp.mean(vector * vector, axis=-1, keepdims=True)
    return vector * lax.rsqrt(meansq + EPSILON) * (1.0 + gain_row)


def rotate(vector, positions):
    half_dim = vector.shape[-1] // 2
    exponent = jnp.arange(half_dim, dtype=jnp.float32) * (-2.0 / vector.shape[-1])
    frequency = jnp.power(jnp.float32(10000.0), exponent)
    angles = positions.astype(jnp.float32)[:, None, None] * frequency
    cosine = jnp.cos(angles)
    sine_term = jnp.sin(angles)
    front_half = vector[..., :half_dim]
    back_half = vector[..., half_dim:]
    return jnp.concatenate(
        [front_half * cosine - back_half * sine_term, back_half * cosine + front_half * sine_term],
        axis=-1,
    )


def capped(raw_scores):
    return SOFTCAP * jnp.tanh(raw_scores / SOFTCAP)


def round_back(vector):
    return lax.optimization_barrier(vector.astype(jnp.bfloat16)).astype(jnp.float32)


def pick_slot(vector, my_group, my_slot):
    inner = lax.dynamic_index_in_dim(vector, my_group, 0, False)
    return lax.dynamic_index_in_dim(inner, my_slot, 1, False)


def take_pages(page_block, page_order):
    return jnp.take(page_block, page_order, axis=2)


def project_rows(left, weight_rows):
    return jnp.einsum("bd,cd->bc", left, weight_rows, preferred_element_type=jnp.float32)


def on_device(
    hidden_in,
    prefill_cache,
    lengths,
    page_table,
    qkv_weight,
    out_weight,
    gate_up_weight,
    down_weight,
    norm_gains,
):
    devices = lax.axis_size(TP)
    my_index = lax.axis_index(TP)
    batch_rows = hidden_in.shape[0]
    groups = devices // PREFILL_TP
    per_group = batch_rows // groups
    local_heads = KV_HEADS // PREFILL_TP
    head_share = HEADS // KV_HEADS
    layer_count = prefill_cache.shape[1]
    page_width = prefill_cache.shape[5]
    score_scale = (D / HEADS) ** (-0.5)
    q_cols = HEADS * HEAD_DIM
    k_cols = KV_HEADS * HEAD_DIM
    my_group = my_index // PREFILL_TP
    my_slot = my_index % PREFILL_TP
    group_rows = lax.dynamic_slice_in_dim(page_table, my_group * per_group, per_group, 0)
    group_lengths = lax.dynamic_slice_in_dim(lengths, my_group * per_group, per_group, 0)
    local_cache = prefill_cache[0]
    page_ids = jnp.arange(devices, dtype=jnp.int32)
    onehot = (group_rows[:, :, None] == page_ids[None, None, :]).astype(jnp.int32)
    inverse = jnp.sum(onehot * page_ids[None, :, None], axis=1)
    arranged = jax.vmap(take_pages, in_axes=(2, 0), out_axes=2)(local_cache, inverse)
    relaid = exchange_by_chip(arranged, (("tp_0", "tp_1"), "tp_2"), (1, 0), 3, 3)
    relaid = relaid.reshape(
        layer_count, 2, per_group, groups, PREFILL_TP, page_width, local_heads, HEAD_DIM
    )
    decode_local = relaid.transpose(0, 1, 3, 2, 5, 4, 6, 7).reshape(
        layer_count, 2, batch_rows, page_width, k_cols
    )
    my_pos = my_index * page_width + jnp.arange(page_width, dtype=jnp.int32)
    fresh_slot = my_pos[None, :] == lengths[:, None]
    kept_cache = local_cache.reshape(
        layer_count, 2, per_group, devices, page_width, local_heads, HEAD_DIM
    )
    cache_pos = (
        group_rows[:, :, None] * page_width + jnp.arange(page_width, dtype=jnp.int32)[None, None, :]
    )
    kept_visible = cache_pos < group_lengths[:, None, None]
    stream = hidden_in
    normed = rms_scale(stream, norm_gains[0, 0]).astype(jnp.bfloat16)
    column_part = project_rows(normed, qkv_weight[0]).astype(jnp.bfloat16)
    projected = gather_axes(column_part, (("tp_0", "tp_1"), "tp_2"), (0, 1), 1)
    queries = rotate(
        projected[:, :q_cols].astype(jnp.float32).reshape(batch_rows, HEADS, HEAD_DIM), lengths
    ).astype(jnp.bfloat16)
    new_key = rotate(
        projected[:, q_cols : q_cols + k_cols]
        .astype(jnp.float32)
        .reshape(batch_rows, KV_HEADS, HEAD_DIM),
        lengths,
    ).astype(jnp.bfloat16)
    new_value = projected[:, q_cols + k_cols :]
    key_layer = jnp.where(
        fresh_slot[:, :, None], new_key.reshape(batch_rows, 1, k_cols), decode_local[0, 0]
    )
    value_layer = jnp.where(
        fresh_slot[:, :, None], new_value.reshape(batch_rows, 1, k_cols), decode_local[0, 1]
    )
    written = [jnp.stack([key_layer, value_layer], axis=0)]
    flat_q = queries.reshape(batch_rows, KV_HEADS, head_share, HEAD_DIM)
    flat_k = new_key.reshape(batch_rows, KV_HEADS, 1, HEAD_DIM)
    flat_v = new_value.reshape(batch_rows, KV_HEADS, 1, HEAD_DIM)
    own_weight = jnp.exp(
        capped(
            jnp.sum(flat_q.astype(jnp.float32) * flat_k.astype(jnp.float32), axis=-1) * score_scale
        )
    )
    own_term = round_back(own_weight)[..., None] * flat_v.astype(jnp.float32)
    shaped_q = flat_q.reshape(groups, per_group, PREFILL_TP, local_heads, head_share, HEAD_DIM)
    shaped_own = own_weight.reshape(groups, per_group, PREFILL_TP, local_heads, head_share)
    shaped_term = own_term.reshape(groups, per_group, PREFILL_TP, local_heads, head_share, HEAD_DIM)
    my_queries = pick_slot(shaped_q, my_group, my_slot)
    cached_keys = kept_cache[0, 0]
    cached_values = kept_cache[0, 1]
    raw_scores = (
        jnp.einsum("ramd,rjcad->ramjc", my_queries, cached_keys, preferred_element_type=jnp.float32)
        * score_scale
    )
    weights = jnp.where(kept_visible[:, None, None, :, :], jnp.exp(capped(raw_scores)), 0.0)
    numerator = jnp.einsum(
        "ramjc,rjcad->ramd",
        weights.astype(jnp.bfloat16),
        cached_values,
        preferred_element_type=jnp.float32,
    )
    numerator = numerator + pick_slot(shaped_term, my_group, my_slot)
    denominator = jnp.sum(weights, axis=(-2, -1)) + pick_slot(shaped_own, my_group, my_slot)
    mine = (
        (numerator / denominator[..., None])
        .astype(jnp.bfloat16)
        .reshape(1, per_group, local_heads * head_share * HEAD_DIM)
    )
    gathered = lax.all_gather(mine, TP, axis=0, tiled=True)
    attended = (
        gathered.reshape(groups, PREFILL_TP, per_group, local_heads * head_share * HEAD_DIM)
        .transpose(0, 2, 1, 3)
        .reshape(batch_rows, q_cols)
    )
    mixed_part = project_rows(attended, out_weight[0]).astype(jnp.bfloat16)
    mixed_out = gather_axes(mixed_part, (("tp_0", "tp_1"), "tp_2"), (0, 1), 1)
    stream = stream + rms_scale(mixed_out.astype(jnp.float32), norm_gains[0, 1])
    ffn_in = rms_scale(stream, norm_gains[0, 2]).astype(jnp.bfloat16)
    gate_proj = project_rows(ffn_in, gate_up_weight[0, 0])
    up_proj = project_rows(ffn_in, gate_up_weight[0, 1])
    active = (jax.nn.gelu(gate_proj, approximate=True) * up_proj).astype(jnp.bfloat16)
    branch = jnp.dot(active, down_weight[0], preferred_element_type=jnp.float32)
    column_count = branch.shape[1] // devices
    portion = summed_rows(branch.astype(jnp.bfloat16), TP, (2, 0, 1), 1).astype(jnp.float32)
    squares = one_axis_at_a_time(jnp.sum(portion * portion, axis=-1), TP)
    gain_part = lax.dynamic_slice_in_dim(norm_gains[0, 3], my_index * column_count, column_count, 0)
    stream_part = lax.dynamic_slice_in_dim(stream, my_index * column_count, column_count, 1)
    result = stream_part + portion * lax.rsqrt(squares[:, None] / D + EPSILON) * (1.0 + gain_part)
    decode_cache = jnp.stack(written, axis=0)[None]
    return (result, decode_cache)


def solution(mesh):
    torus = Mesh(mesh.devices.reshape(mesh.shape["grp"], 8, 8, 2), ("grp", "tp_0", "tp_1", "tp_2"))
    return jax.shard_map(
        on_device,
        mesh=torus,
        in_specs=(
            P("grp", None),
            P(TP, None, None, "grp", None, None, None),
            P("grp"),
            P("grp", None),
            P(None, TP, None),
            P(None, TP, None),
            P(None, None, TP, None),
            P(None, TP, None),
            P(),
        ),
        out_specs=(P("grp", TP), P(TP, None, None, "grp", None, None)),
        check_vma=False,
    )
```

profile of v0, /device:TPU:513, one launch (start us, length us, event | category | flops | bytes accessed | tf_op | source)
XLA Modules:
  0.0 438.4 jit_solution(14225029123569597473)
XLA Ops:
  8.2 2.8 gather_fusion
  11.5 25.5 %all_to_all.10 = bf16[64,2,1,2,2,1,8,256]{7,6,0,4,3,5,2,1:T(8,128)(2,1)S(1)} all-to-all(bf16[64,2,1,2,2,1,8,256]{7,6,0,4,3,5,2,1:T(8,128)(2,1)S(1)} %copy.124), channel_id=1, replica_groups=mesh['grp'=2,'tp_0'=8,'tp_1'=8,'tp_2'=2] {'tp_2'}, dimensions={1} | all-to-all | bytes 4194304 | tf_op jit(solution)/shard_map/all_to_all | solution.py:32
  38.6 7.3 %all-to-all-start.1 = ((bf16[64,2,1,2,2,1,8,256]{7,6,1,4,3,5,2,0:T(8,128)(2,1)}), bf16[64,2,1,2,2,1,8,256]{7,6,1,4,3,5,2,0:T(8,128)(2,1)}, u32[]{:S(2)}, u32[]{:S(2)}) async-start(bf16[64,2,1,2,2,1,8,256]{7,6,1,4,3,5,2,0:T(8,128)(2,1)} %copy.125), calls=%async_computation.4 | async-start | bytes 4194304 | tf_op jit(solution)/shard_map/all_to_all | solution.py:32
  47.9 83.7 %all-gather = bf16[2048,64]{1,0:T(8,128)(2,1)S(1)} all-gather(bf16[32,64]{1,0:T(8,128)(2,1)S(1)} %convolution_convert_fusion.1), channel_id=2, replica_groups=mesh['grp'=2,'tp_0'=8,'tp_1'=8,'tp_2'=2] {'tp_0','tp_1'}, dimensions={0}, use_global_device_ids=true | all-gather | bytes 266240 | tf_op jit(solution)/shard_map/all_gather | solution.py:45
  131.7 13.7 %all_gather.16 = bf16[128,32,64]{2,1,0:T(8,128)(2,1)S(1)} all-gather(bf16[64,32,64]{2,1,0:T(8,128)(2,1)S(1)} %bitcast.167), channel_id=1, replica_groups=mesh['grp'=2,'tp_0'=8,'tp_1'=8,'tp_2'=2] {'tp_2'}, dimensions={0}, use_global_device_ids=true | all-gather | bytes 786432 | tf_op jit(solution)/shard_map/all_gather | solution.py:45
  149.3 2.9 reshape.346
  152.1 1.8 convert_bitcast_fusion.1
  153.9 1.8 fusion.55
  163.8 2.3 copy.116
  169.2 47.3 %all_gather.17 = bf16[128,2,512]{2,1,0:T(2,128)(2,1)S(1)} all-gather(bf16[1,2,512]{2,1,0:T(2,128)(2,1)S(1)} %reshape.351), channel_id=1, replica_groups=mesh['grp'=2,'tp_0'=8,'tp_1'=8,'tp_2'=2] {'tp_0','tp_1','tp_2'}, dimensions={0}, use_global_device_ids=true | all-gather | bytes 264192 | tf_op jit(solution)/shard_map/all_gather | solution.py:220
  216.9 38.2 %all-gather.1 = bf16[2048,36]{1,0:T(8,128)(2,1)S(1)} all-gather(bf16[32,36]{1,0:T(8,128)(2,1)S(1)} %convolution_convert_fusion.2), channel_id=3, replica_groups=mesh['grp'=2,'tp_0'=8,'tp_1'=8,'tp_2'=2] {'tp_0','tp_1'}, dimensions={0}, use_global_device_ids=true | all-gather | bytes 149760 | tf_op jit(solution)/shard_map/all_gather | solution.py:45
  255.2 14.1 %all_gather.19 = bf16[128,32,36]{2,1,0:T(8,128)(2,1)S(1)} all-gather(bf16[64,32,36]{2,1,0:T(8,128)(2,1)S(1)} %bitcast.168), channel_id=1, replica_groups=mesh['grp'=2,'tp_0'=8,'tp_1'=8,'tp_2'=2] {'tp_2'}, dimensions={0}, use_global_device_ids=true | all-gather | bytes 442368 | tf_op jit(solution)/shard_map/all_gather | solution.py:45
  269.5 2.9 copy.121
  272.5 3.3 reshape.368
  278.1 2.5 convolution_convert_fusion
  280.6 2.8 reshape.355
  285.2 16.1 %reduce-scatter.4.cloned.1.call-done = bf16[64,32,36]{2,1,0:T(8,128)(2,1)} async-done(((bf16[128,32,36]{2,1,0:T(8,128)(2,1)}), bf16[64,32,36]{2,1,0:T(8,128)(2,1)}) %reduce-scatter.4.cloned.1.call-update) | async-done | bytes 147472 | tf_op jit(solution)/shard_map/reduce_scatter | solution.py:62
  302.2 35.5 %reduce-scatter.6.cloned.1.call-done = bf16[8,32,36]{2,1,0:T(8,128)(2,1)} async-done(((bf16[64,32,36]{2,1,0:T(8,128)(2,1)}), bf16[8,32,36]{2,1,0:T(8,128)(2,1)}) %reduce-scatter.6.cloned.1.call-update) | async-done | bytes 18448 | tf_op jit(solution)/shard_map/reduce_scatter | solution.py:62
  339.1 38.0 %reduce-scatter.8.cloned.1.call-done = bf16[1,32,36]{2,1,0:T(8,128)(2,1)} async-done(((bf16[8,32,36]{2,1,0:T(8,128)(2,1)}), bf16[1,32,36]{2,1,0:T(8,128)(2,1)}) %reduce-scatter.8.cloned.1.call-update) | async-done | bytes 2320 | tf_op jit(solution)/shard_map/reduce_scatter | solution.py:62
  378.0 13.2 %psum.21 = f32[32]{0:T(128)S(1)} all-reduce(f32[32]{0:T(128)S(1)} %fusion.38), channel_id=1, replica_groups=mesh['grp'=2,'tp_0'=8,'tp_1'=8,'tp_2'=2] {'tp_0'}, use_global_device_ids=true, to_apply=%region_9.10 | all-reduce | flops 32 | bytes 256 | tf_op jit(solution)/shard_map/psum | solution.py:73
  391.1 12.0 %psum.22 = f32[32]{0:T(128)S(1)} all-reduce(f32[32]{0:T(128)S(1)} %psum.21), channel_id=1, replica_groups=mesh['grp'=2,'tp_0'=8,'tp_1'=8,'tp_2'=2] {'tp_1'}, use_global_device_ids=true, to_apply=%region_10.11 | all-reduce | flops 32 | bytes 256 | tf_op jit(solution)/shard_map/psum | solution.py:73
  403.1 15.9 %psum.23 = f32[32]{0:T(128)S(1)} all-reduce(f32[32]{0:T(128)S(1)} %psum.22), channel_id=1, replica_groups=mesh['grp'=2,'tp_0'=8,'tp_1'=8,'tp_2'=2] {'tp_2'}, use_global_device_ids=true, to_apply=%region_11.12 | all-reduce | flops 32 | bytes 256 | tf_op jit(solution)/shard_map/psum | solution.py:73
  422.2 3.5 copy.127
  425.8 3.3 reshape.361
  (97 shorter events, 33.7 us)
Async XLA Ops:
  7.2 270.9 %copy-start = (bf16[1,144,4608]{2,1,0:T(8,128)(2,1)S(1)}, bf16[1,144,4608]{2,1,0:T(8,128)(2,1)}, u32[]{:S(2)}) copy-start(bf16[1,144,4608]{2,1,0:T(8,128)(2,1)} %param.16) | copy-start | bytes 3981316
  38.6 7.5 %copy-start.13 = (s32[32]{0:T(128)S(1)}, s32[32]{0:T(128)}, u32[]{:S(2)}) copy-start(s32[32]{0:T(128)} %param.11) | copy-start | bytes 388
  38.6 7.6 %copy-start.12 = (f32[1,4,4608]{2,1,0:T(4,128)S(1)}, f32[1,4,4608]{2,1,0:T(4,128)}, u32[]{:S(2)}) copy-start(f32[1,4,4608]{2,1,0:T(4,128)} %param.17) | copy-start | bytes 221188
  38.6 8.8 %copy-start.2 = (f32[32,4608]{1,0:T(8,128)S(1)}, f32[32,4608]{1,0:T(8,128)}, u32[]{:S(2)}) copy-start(f32[32,4608]{1,0:T(8,128)} %param.9) | copy-start | bytes 1769476
  38.6 9.0 %copy-start.6 = (bf16[1,64,4608]{2,1,0:T(8,128)(2,1)S(1)}, bf16[1,64,4608]{2,1,0:T(8,128)(2,1)}, u32[]{:S(2)}) copy-start(bf16[1,64,4608]{2,1,0:T(8,128)(2,1)} %param.13) | copy-start | bytes 1769476
  38.6 381.9 %all-to-all-start.1 = ((bf16[64,2,1,2,2,1,8,256]{7,6,1,4,3,5,2,0:T(8,128)(2,1)}), bf16[64,2,1,2,2,1,8,256]{7,6,1,4,3,5,2,0:T(8,128)(2,1)}, u32[]{:S(2)}, u32[]{:S(2)}) async-start(bf16[64,2,1,2,2,1,8,256]{7,6,1,4,3,5,2,0:T(8,128)(2,1)} %copy.125), calls=%async_computation.4 | async-start | bytes 4194304 | tf_op jit(solution)/shard_map/all_to_all | solution.py:32
  45.9 255.4 %reduce-scatter.4.cloned.1.call-start = ((), (), s32[]{:S(2)}) async-start(), calls=%async_computation.5 | async-start | bytes 1572864 | tf_op jit(solution)/shard_map/reduce_scatter | solution.py:62
  149.2 6.5 %copy-start.1 = (bf16[1,1,2,2,128,8,256]{6,5,4,3,2,1,0:T(8,128)(2,1)S(1)}, bf16[1,1,2,2,128,8,256]{6,5,4,3,2,1,0:T(8,128)(2,1)}, u32[]{:S(2)}) copy-start(bf16[1,1,2,2,128,8,256]{6,5,4,3,2,1,0:T(8,128)(2,1)} %param.10) | copy-start | bytes 6291460
  161.1 5.4 %copy-start.4 = (bf16[1,1,2,128,8,2,128]{6,4,5,3,2,1,0:T(8,128)(2,1)S(1)}, bf16[1,1,2,128,8,2,128]{6,4,5,3,2,1,0:T(8,128)(2,1)}, u32[]{:S(2)}) copy-start(bf16[1,1,2,128,8,2,128]{6,4,5,3,2,1,0:T(8,128)(2,1)} %get-tuple-element.13) | copy-start | bytes 3145732
  166.5 50.2 %copy-start.9 = (bf16[1,36,4096]{2,1,0:T(8,128)(2,1)S(1)}, bf16[1,36,4096]{2,1,0:T(8,128)(2,1)}, u32[]{:S(2)}) copy-start(bf16[1,36,4096]{2,1,0:T(8,128)(2,1)} %param.14) | copy-start | bytes 884740
  272.5 3.7 copy-start.3
  275.7 1.8 copy-start.5
  275.7 1.8 copy-start.10
  276.2 1.9 copy-start.11
  283.4 18.1 %copy-start.14 = (s32[32]{0:T(128)S(1)}, s32[32]{0:T(128)}, u32[]{:S(2)}) copy-start(s32[32]{0:T(128)} %param.11) | copy-start | bytes 388
  283.4 55.0 %copy-start.8 = (bf16[32,16,128]{2,1,0:T(8,128)(2,1)S(1)}, bf16[32,16,128]{2,1,0:T(8,128)(2,1)}, u32[]{:S(2)}) copy-start(bf16[32,16,128]{2,1,0:T(8,128)(2,1)} %get-tuple-element.8) | copy-start | bytes 393220
  285.1 52.5 %reduce-scatter.6.cloned.1.call-start = ((), (), s32[]{:S(2)}) async-start(), calls=%async_computation.6 | async-start | bytes 589824 | tf_op jit(solution)/shard_map/reduce_scatter | solution.py:62
  301.4 75.7 %reduce-scatter.8.cloned.1.call-start = ((), (), s32[]{:S(2)}) async-start(), calls=%async_computation.7 | async-start | bytes 73728 | tf_op jit(solution)/shard_map/reduce_scatter | solution.py:62
  425.8 3.3 copy-start.7
Sparse Core Ops, SparseCore 0:
  285.3 16.0 reduce-scatter.3
  303.9 33.6 reduce-scatter.5
  340.1 36.9 reduce-scatter.7
where the time goes:
time: 439 us; the launch traced here: 438 us
  blocking collectives  264 us (60%)
  waiting for transfers between devices  89.8 us (20%)
  local copies, waits for them, and re-layouts  40.1 us (9%)
  other arithmetic  17.5 us (4%)
  between operations  14.2 us (3%)
  starting transfers between devices  7.52 us (2%)
  matrix products  5.66 us (1%)
    all_gather x4, blocking collectives, gather_in_order(): tiles = lax.all_gather(tiles, axes[k], axis=0, tiled=True)  150 us
    reduce_scatter x3, waiting for transfers between devices, own_block(): tiles = lax.psum_scatter(tiles, axes[k], scatter_dimension=0, tiled=True)  89.6 us
    all_gather x1, blocking collectives, on_device(): gathered = lax.all_gather(mine, TP, axis=0, tiled=True)  47.3 us
    psum x3, blocking collectives, one_axis_at_a_time(): shard = lax.psum(shard, axis)  41.1 us
    all_to_all x1, blocking collectives, turned_blocks(): lax.all_to_all(tiles, axes[k], split_axis=k, concat_axis=k, tiled=True)  25.5 us
  transfers between devices with their start and end apart: 4, of which 3 were waited for; matrix products, arithmetic and copies ran while one was open for 10% of the time, Pallas kernels for 0%

commit v1 on v0

--- a/solution.py
+++ b/solution.py
@@ -42,7 +42,9 @@
 def gather_in_order(shard, axes, turns):
     tiles = shard[None]
     for k in turns:
-        tiles = lax.all_gather(tiles, axes[k], axis=0, tiled=True)
+        tiles = jnp.concatenate(
+            lax.all_to_all(jnp.stack([tiles] * lax.axis_size(axes[k])), axes[k], 0, 0), axis=0
+        )
     held = [lax.axis_size(axes[k]) for k in reversed(turns)]
     tiles = tiles.reshape(*held, *shard.shape)
     turned = sorted(range(len(turns)), key=lambda place: turns[len(turns) - 1 - place])

time: 439 us -> 392 us (0.89)
  blocking collectives: 264 us -> 109 us
  local copies, waits for them, and re-layouts: 40.1 us -> 76.5 us
  starting transfers between devices: 7.52 us -> 43.7 us
  other arithmetic: 17.5 us -> 31.1 us
  waiting for transfers between devices: 89.8 us -> 103 us
  matrix products: 5.66 us -> 12.6 us
    all_gather x4 -> x0, blocking collectives: 150 us -> none  [gather_in_order(): tiles = lax.all_gather(tiles, axes[k], axis=0, tiled=True)]
    all_to_all x0 -> x2, starting transfers between devices: none -> 32.6 us  [gather_in_order(): lax.all_to_all(jnp.stack([tiles] * lax.axis_size(axes[k])), axes[k], 0, 0)]
    unnamed x34 -> x32, local copies, waits for them, and re-layouts: 3.03 us -> 18 us
    all_to_all x0 -> x2, waiting for transfers between devices: none -> 10.2 us  [gather_in_order(): lax.all_to_all(jnp.stack([tiles] * lax.axis_size(axes[k])), axes[k], 0, 0)]
    all_to_all x1 -> x2, blocking collectives: 25.5 us -> 18.1 us  [gather_in_order(): lax.all_to_all(jnp.stack([tiles] * lax.axis_size(axes[k])), axes[k], 0, 0)]
    convert_element_type x2 -> x3, local copies, waits for them, and re-layouts: 6.21 us -> 11.9 us  [on_device(): stream = stream + rms_scale(mixed_out.astype(jnp.float32), norm_gains[0, 1])]
    all_to_all x1 -> x2, starting transfers between devices: 7.33 us -> 10.7 us  [turned_blocks(): lax.all_to_all(tiles, axes[k], split_axis=k, concat_axis=k, tiled=True)]
  transfers between devices with their start and end apart: 4 -> 7, of which waited for: 3 -> 5; matrix products, arithmetic and copies ran while one was open for 10% -> 25% of each run, Pallas kernels for 0% -> 0%
where the time goes in v1:
time: 392 us; the launch traced here: 390 us
  blocking collectives  109 us (28%)
  waiting for transfers between devices  103 us (26%)
  local copies, waits for them, and re-layouts  76.5 us (20%)
  starting transfers between devices  43.7 us (11%)
  other arithmetic  31.1 us (8%)
  between operations  14.1 us (4%)
  matrix products  12.6 us (3%)
    reduce_scatter x3, waiting for transfers between devices, own_block(): tiles = lax.psum_scatter(tiles, axes[k], scatter_dimension=0, tiled=True)  93.1 us
    all_gather x1, blocking collectives, on_device(): gathered = lax.all_gather(mine, TP, axis=0, tiled=True)  48 us
    psum x3, blocking collectives, one_axis_at_a_time(): shard = lax.psum(shard, axis)  42.6 us
    all_to_all x2, starting transfers between devices, gather_in_order(): lax.all_to_all(jnp.stack([tiles] * lax.axis_size(axes[k])), axes[k], 0, 0)  32.6 us
    all_to_all x2, blocking collectives, gather_in_order(): lax.all_to_all(jnp.stack([tiles] * lax.axis_size(axes[k])), axes[k], 0, 0)  18.1 us
    unnamed x32, local copies, waits for them, and re-layouts  18 us
    convert_element_type x3, local copies, waits for them, and re-layouts, on_device(): stream = stream + rms_scale(mixed_out.astype(jnp.float32), norm_gains[0, 1])  11.9 us
    all_to_all x2, starting transfers between devices, turned_blocks(): lax.all_to_all(tiles, axes[k], split_axis=k, concat_axis=k, tiled=True)  10.7 us
  transfers between devices with their start and end apart: 7, of which 5 were waited for; matrix products, arithmetic and copies ran while one was open for 25% of the time, Pallas kernels for 0%

profile of v1, /device:TPU:513, one launch (start us, length us, event | category | flops | bytes accessed | tf_op | source)
XLA Modules:
  0.0 390.1 jit_solution(8180587352634745863)
XLA Ops:
  15.4 21.8 %all-to-all-start = ((bf16[64,2,1024]{2,1,0:T(2,128)(2,1)}), bf16[64,2,1024]{2,1,0:T(2,128)(2,1)}, u32[]{:S(2)}, u32[]{:S(2)}) async-start(bf16[64,2,1024]{2,1,0:T(2,128)(2,1)} %reshape.382), calls=%async_computation | async-start | bytes 524288 | tf_op jit(solution)/shard_map/all_to_all | solution.py:46
  50.9 11.4 %all_to_all.30 = bf16[2,2,65536]{2,1,0:T(2,128)(2,1)} all-to-all(bf16[2,2,65536]{2,1,0:T(2,128)(2,1)S(1)} %reshape.384), channel_id=1, replica_groups=mesh['grp'=2,'tp_0'=8,'tp_1'=8,'tp_2'=2] {'tp_2'}, dimensions={0} | all-to-all | bytes 1048576 | tf_op jit(solution)/shard_map/all_to_all | solution.py:46
  62.3 4.1 %all-to-all-start.4 = ((bf16[64,2,1,2,2,1,8,256]{7,6,0,4,3,5,2,1:T(8,128)(2,1)}), bf16[64,2,1,2,2,1,8,256]{7,6,0,4,3,5,2,1:T(8,128)(2,1)S(1)}, u32[]{:S(2)}, u32[]{:S(2)}) async-start(bf16[64,2,1,2,2,1,8,256]{7,6,0,4,3,5,2,1:T(8,128)(2,1)} %copy.151), calls=%async_computation.7 | async-start | bytes 4194304 | tf_op jit(solution)/shard_map/all_to_all | solution.py:32
  71.7 2.7 reshape.343
  90.1 3.3 copy.141
  105.9 48.0 %all_gather.3 = bf16[128,2,512]{2,1,0:T(2,128)(2,1)S(1)} all-gather(bf16[1,2,512]{2,1,0:T(2,128)(2,1)} %reshape.348), channel_id=1, replica_groups=mesh['grp'=2,'tp_0'=8,'tp_1'=8,'tp_2'=2] {'tp_0','tp_1','tp_2'}, dimensions={0}, use_global_device_ids=true | all-gather | bytes 264192 | tf_op jit(solution)/shard_map/all_gather | solution.py:222
  158.6 10.8 %all-to-all-start.2 = ((bf16[64,2,576]{2,1,0:T(2,128)(2,1)}), bf16[64,2,576]{2,1,0:T(2,128)(2,1)}, u32[]{:S(2)}, u32[]{:S(2)}) async-start(bf16[64,2,576]{2,1,0:T(2,128)(2,1)} %reshape.386), calls=%async_computation.2 | async-start | bytes 327680 | tf_op jit(solution)/shard_map/all_to_all | solution.py:46
  171.0 8.8 %all-to-all-done.2 = bf16[64,2,576]{2,1,0:T(2,128)(2,1)} async-done(((bf16[64,2,576]{2,1,0:T(2,128)(2,1)}), bf16[64,2,576]{2,1,0:T(2,128)(2,1)}, u32[]{:S(2)}, u32[]{:S(2)}) %all-to-all-start.2) | async-done | bytes 147488 | tf_op jit(solution)/shard_map/all_to_all | solution.py:46
  183.0 6.7 %all_to_all.31 = bf16[2,2,36864]{2,1,0:T(2,128)(2,1)} all-to-all(bf16[2,2,36864]{2,1,0:T(2,128)(2,1)S(1)} %reshape.388), channel_id=1, replica_groups=mesh['grp'=2,'tp_0'=8,'tp_1'=8,'tp_2'=2] {'tp_2'}, dimensions={0} | all-to-all | bytes 589824 | tf_op jit(solution)/shard_map/all_to_all | solution.py:46
  189.7 6.6 %all-to-all-start.5 = ((bf16[64,2,1,2,2,1,8,256]{7,6,1,4,3,5,2,0:T(8,128)(2,1)}), bf16[64,2,1,2,2,1,8,256]{7,6,1,4,3,5,2,0:T(8,128)(2,1)S(1)}, u32[]{:S(2)}, u32[]{:S(2)}) async-start(bf16[64,2,1,2,2,1,8,256]{7,6,1,4,3,5,2,0:T(8,128)(2,1)} %copy.152), calls=%async_computation.8 | async-start | bytes 4194304 | tf_op jit(solution)/shard_map/all_to_all | solution.py:32
  200.8 3.7 copy.147
  204.5 4.1 %copy.148 = f32[32,128,36]{2,1,0:T(8,128)} copy(f32[32,128,36]{2,0,1:T(8,128)} %bitcast.154) | data formatting | bytes 1179648 | tf_op jit(solution)/shard_map/convert_element_type | solution.py:230
  208.6 4.0 %reshape.364 = f32[32,4608]{1,0:T(8,128)} reshape(f32[32,128,36]{2,1,0:T(8,128)} %copy.148) | data formatting | bytes 1179648 | tf_op jit(solution)/shard_map/convert_element_type | solution.py:230
  218.9 3.4 convolution_convert_fusion
  222.3 4.7 %reshape.351 = bf16[32,128,36]{2,1,0:T(8,128)(2,1)} reshape(bf16[32,4608]{1,0:T(8,128)(2,1)} %convolution_convert_fusion) | data formatting | bytes 589824 | tf_op jit(solution)/shard_map/reshape | solution.py:19
  227.0 2.9 copy.149
  230.0 21.9 %reduce-scatter.4.cloned.1.call-done = bf16[64,32,36]{2,1,0:T(8,128)(2,1)} async-done(((bf16[128,32,36]{2,1,0:T(8,128)(2,1)}), bf16[64,32,36]{2,1,0:T(8,128)(2,1)}) %reduce-scatter.4.cloned.1.call-update) | async-done | bytes 147472 | tf_op jit(solution)/shard_map/reduce_scatter | solution.py:64
  253.7 34.5 %reduce-scatter.6.cloned.1.call-done = bf16[8,32,36]{2,1,0:T(8,128)(2,1)} async-done(((bf16[64,32,36]{2,1,0:T(8,128)(2,1)}), bf16[8,32,36]{2,1,0:T(8,128)(2,1)}) %reduce-scatter.6.cloned.1.call-update) | async-done | bytes 18448 | tf_op jit(solution)/shard_map/reduce_scatter | solution.py:64
  291.1 36.7 %reduce-scatter.8.cloned.1.call-done = bf16[1,32,36]{2,1,0:T(8,128)(2,1)} async-done(((bf16[8,32,36]{2,1,0:T(8,128)(2,1)}), bf16[1,32,36]{2,1,0:T(8,128)(2,1)}) %reduce-scatter.8.cloned.1.call-update) | async-done | bytes 2320 | tf_op jit(solution)/shard_map/reduce_scatter | solution.py:64
  329.1 13.7 %psum.21 = f32[32]{0:T(128)} all-reduce(f32[32]{0:T(128)} %fusion.38), channel_id=1, replica_groups=mesh['grp'=2,'tp_0'=8,'tp_1'=8,'tp_2'=2] {'tp_0'}, use_global_device_ids=true, to_apply=%region_9.10 | all-reduce | flops 32 | bytes 256 | tf_op jit(solution)/shard_map/psum | solution.py:75
  342.7 12.9 %psum.22 = f32[32]{0:T(128)} all-reduce(f32[32]{0:T(128)} %psum.21), channel_id=1, replica_groups=mesh['grp'=2,'tp_0'=8,'tp_1'=8,'tp_2'=2] {'tp_1'}, use_global_device_ids=true, to_apply=%region_10.11 | all-reduce | flops 32 | bytes 256 | tf_op jit(solution)/shard_map/psum | solution.py:75
  355.7 16.0 %psum.23 = f32[32]{0:T(128)} all-reduce(f32[32]{0:T(128)} %psum.22), channel_id=1, replica_groups=mesh['grp'=2,'tp_0'=8,'tp_1'=8,'tp_2'=2] {'tp_2'}, use_global_device_ids=true, to_apply=%region_11.12 | all-reduce | flops 32 | bytes 256 | tf_op jit(solution)/shard_map/psum | solution.py:75
  373.9 3.5 copy.154
  377.5 3.3 reshape.357
  (103 shorter events, 86.5 us)
Async XLA Ops:
  7.2 211.7 %copy-start = (bf16[1,144,4608]{2,1,0:T(8,128)(2,1)S(1)}, bf16[1,144,4608]{2,1,0:T(8,128)(2,1)}, u32[]{:S(2)}) copy-start(bf16[1,144,4608]{2,1,0:T(8,128)(2,1)} %param.16) | copy-start | bytes 3981316
  7.2 30.1 %copy-start.9 = (s32[32]{0:T(128)S(1)}, s32[32]{0:T(128)}, u32[]{:S(2)}) copy-start(s32[32]{0:T(128)} %param.11) | copy-start | bytes 388
  7.2 31.0 %copy-start.1 = (bf16[1,1,2,2,128,8,256]{6,5,4,3,2,1,0:T(8,128)(2,1)S(1)}, bf16[1,1,2,2,128,8,256]{6,5,4,3,2,1,0:T(8,128)(2,1)}, u32[]{:S(2)}) copy-start(bf16[1,1,2,2,128,8,256]{6,5,4,3,2,1,0:T(8,128)(2,1)} %param.10) | copy-start | bytes 6291460
  15.4 33.1 %all-to-all-start = ((bf16[64,2,1024]{2,1,0:T(2,128)(2,1)}), bf16[64,2,1024]{2,1,0:T(2,128)(2,1)}, u32[]{:S(2)}, u32[]{:S(2)}) async-start(bf16[64,2,1024]{2,1,0:T(2,128)(2,1)} %reshape.382), calls=%async_computation | async-start | bytes 524288 | tf_op jit(solution)/shard_map/all_to_all | solution.py:46
  62.3 96.3 %all-to-all-start.4 = ((bf16[64,2,1,2,2,1,8,256]{7,6,0,4,3,5,2,1:T(8,128)(2,1)}), bf16[64,2,1,2,2,1,8,256]{7,6,0,4,3,5,2,1:T(8,128)(2,1)S(1)}, u32[]{:S(2)}, u32[]{:S(2)}) async-start(bf16[64,2,1,2,2,1,8,256]{7,6,0,4,3,5,2,1:T(8,128)(2,1)} %copy.151), calls=%async_computation.7 | async-start | bytes 4194304 | tf_op jit(solution)/shard_map/all_to_all | solution.py:32
  80.0 2.5 copy-start.6
  80.0 2.5 copy-start.7
  82.5 1.0 copy-start.3
  82.5 1.0 copy-start.4
  158.6 21.2 %all-to-all-start.2 = ((bf16[64,2,576]{2,1,0:T(2,128)(2,1)}), bf16[64,2,576]{2,1,0:T(2,128)(2,1)}, u32[]{:S(2)}, u32[]{:S(2)}) async-start(bf16[64,2,576]{2,1,0:T(2,128)(2,1)} %reshape.386), calls=%async_computation.2 | async-start | bytes 327680 | tf_op jit(solution)/shard_map/all_to_all | solution.py:46
  189.7 184.1 %all-to-all-start.5 = ((bf16[64,2,1,2,2,1,8,256]{7,6,1,4,3,5,2,0:T(8,128)(2,1)}), bf16[64,2,1,2,2,1,8,256]{7,6,1,4,3,5,2,0:T(8,128)(2,1)S(1)}, u32[]{:S(2)}, u32[]{:S(2)}) async-start(bf16[64,2,1,2,2,1,8,256]{7,6,1,4,3,5,2,0:T(8,128)(2,1)} %copy.152), calls=%async_computation.8 | async-start | bytes 4194304 | tf_op jit(solution)/shard_map/all_to_all | solution.py:32
  196.2 55.7 %reduce-scatter.4.cloned.1.call-start = ((), (), s32[]{:S(2)}) async-start(), calls=%async_computation.9 | async-start | bytes 1572864 | tf_op jit(solution)/shard_map/reduce_scatter | solution.py:64
  212.6 3.7 copy-start.5
  215.5 0.8 copy-start.2
  215.6 0.8 copy-start.8
  230.0 58.2 %reduce-scatter.6.cloned.1.call-start = ((), (), s32[]{:S(2)}) async-start(), calls=%async_computation.10 | async-start | bytes 589824 | tf_op jit(solution)/shard_map/reduce_scatter | solution.py:64
  252.0 75.7 %reduce-scatter.8.cloned.1.call-start = ((), (), s32[]{:S(2)}) async-start(), calls=%async_computation.11 | async-start | bytes 73728 | tf_op jit(solution)/shard_map/reduce_scatter | solution.py:64
Sparse Core Ops, SparseCore 0:
  230.1 21.7 reduce-scatter.3
  254.5 33.6 reduce-scatter.5
  290.7 37.0 reduce-scatter.7
